TPU v7x, 32 devices: a whole 2x2x4 slice. The times are simulated.
32 devices in a mesh: fit: 2 (over x), comp: 4 (over z), pts: 4 (over y, core).
Axes of the slice: x: 2, y: 2, z: 4, core: 2. Of those that a mesh axis runs over, the one named last changes fastest.
Arguments:
- points: bfloat16 [16384, 1024], P(('fit', 'pts')), parts along dimension 0
- means_init: float32 [32768, 1024], P(('fit', 'comp')), parts along dimension 0
- logw_init: float32 [32768], P(('fit', 'comp')), parts along dimension 0
- inv_temp: float32 [3], replicated
Outputs:
- output 1: float32 [32768, 1024], P(('fit', 'comp')), parts along dimension 0
- output 2: float32 [32768], P(('fit', 'comp')), parts along dimension 0
- output 3: float32 [16384], P(('fit', 'pts')), parts along dimension 0
There are 2 independent parts. A program takes and returns all parts, laid end to end along the dimension named above; an argument that names none is the same for every part.
All inputs are finite; a program needn't handle non-finite values.
Results may differ from a plain program's by a relative error of at most 0.001.
Values are sent between devices in bfloat16 or wider.
A program may use at most 1 GiB of HBM per device.

v0:
```python
import jax
import jax.numpy as jnp
from jax import lax
from jax.sharding import PartitionSpec as P

PRIOR_ALPHA = 1e-3
COUNT_EPS = 1e-6


def solution(mesh):
    row_groups = mesh.shape["pts"]
    comp_groups = mesh.shape["comp"]

    def per_device(points, mean_vecs, log_w, inv_temp):
        n_total = points.shape[0] * row_groups
        k_total = mean_vecs.shape[0] * comp_groups
        x_sq = jnp.einsum("nd,nd->n", points, points, preferred_element_type=jnp.float32)
        log_norm = None
        for sweep_idx in range(inv_temp.shape[0]):
            mean_bf = mean_vecs.astype(jnp.bfloat16)
            mean_sq = jnp.sum(mean_vecs * mean_vecs, axis=1)
            cross_dot = jnp.einsum("nd,kd->nk", points, mean_bf, preferred_element_type=jnp.float32)
            logits = log_w[None, :] - inv_temp[sweep_idx] * (x_sq[:, None] - 2.0 * cross_dot + mean_sq[None, :])
            row_top = lax.pmax(jnp.max(logits, axis=1), "comp")
            exp_total = lax.psum(jnp.sum(jnp.exp(logits - row_top[:, None]), axis=1), "comp")
            log_norm = row_top + jnp.log(exp_total)
            resp_prob = jnp.exp(logits - log_norm[:, None])
            counts = jnp.sum(resp_prob, axis=0)
            stat_sums = jnp.einsum("nk,nd->kd", resp_prob.astype(jnp.bfloat16), points, preferred_element_type=jnp.float32)
            counts, stat_sums = lax.psum((counts, stat_sums), "pts")
            mean_vecs = stat_sums / (counts[:, None] + COUNT_EPS)
            log_w = jnp.log((counts + PRIOR_ALPHA) / (n_total + k_total * PRIOR_ALPHA))
        return mean_vecs, log_w, log_norm

    row_spec = P(("fit", "pts"))
    comp_spec = P(("fit", "comp"))
    return jax.shard_map(
        per_device,
        mesh=mesh,
        in_specs=(P(("fit", "pts"), None), P(("fit", "comp"), None), comp_spec, P()),
        out_specs=(P(("fit", "comp"), None), comp_spec, row_spec),
        check_vma=False,
    )
```

profile of v0, /device:TPU:0, one launch (start us, length us, event | category | flops | bytes accessed | tf_op | source)
XLA Modules:
  0.0 1190.4 jit_solution(894754111481379441)
XLA Ops:
  7.2 0.0 all-reduce.4.cloned.1.call-start
  7.2 1.4 fusion.19
  8.6 3.1 fusion.15
  11.7 6.9 multiply_reduce_fusion.2
  18.6 31.1 %fusion.20 = (f32[2048]{0:T(1024)S(1)}, f32[2048,4096]{1,0:T(8,128)}) fusion(f32[4096]{0:T(1024)S(1)} %multiply_reduce_fusion.2, bf16[2048,1024]{1,0:T(8,128)(2,1)} %param.4, f32[4096,1024]{1,0:T(8,128)} %param.5, f32[2048]{0:T(1024)S(1)} %fusion.15, f32[]{:T(128)} %bitcast, f32[4096]{0:T(1024)} %param.6), kind=kOutput, calls=%fused_computation.42 | convolution fusion | flops 17234393088 | bytes 54575108 | tf_op jit(solution)/shard_map/nd,kd->nk/dot_general | solution.py:22
  49.7 13.7 %pmax.21 = f32[2048]{0:T(1024)S(1)} all-reduce(f32[2048]{0:T(1024)S(1)} %get-tuple-element.12), channel_id=1, replica_groups=mesh['fit'=2,'comp'=4,'pts'=4] {'comp'}, use_global_device_ids=true, to_apply=%region_2.0 | all-reduce | flops 2048 | bytes 16384 | tf_op jit(solution)/shard_map/pmax | solution.py:24
  63.4 13.6 %exponential_reduce_fusion.2 = f32[2048]{0:T(1024)S(1)} fusion(f32[2048,4096]{1,0:T(8,128)} %get-tuple-element.13, f32[2048]{0:T(1024)S(1)} %pmax.21), kind=kLoop, calls=%fused_computation.7 | loop fusion | flops 16775168 | bytes 33570816 | tf_op jit(solution)/shard_map/reduce_sum | solution.py:25
  77.0 9.0 psum.63
  86.1 27.1 %fusion.10 = f32[4096,1024]{1,0:T(8,128)} fusion(bf16[2048,1024]{1,0:T(8,128)(2,1)} %param.4, f32[2048,4096]{1,0:T(8,128)} %get-tuple-element.13, f32[2048]{0:T(1024)S(1)} %log_add_fusion.2), kind=kOutput, calls=%fused_computation.17 | convolution fusion | flops 17196646400 | bytes 54534144 | tf_op jit(solution)/shard_map/nk,nd->kd/dot_general | solution.py:29
  113.2 0.0 all-reduce.4.cloned.1.call-update
  113.2 0.0 all-reduce.6.cloned.1.call-start
  113.2 13.8 %fusion.1 = f32[4096]{0:T(1024)S(1)} fusion(f32[2048,4096]{1,0:T(8,128)} %get-tuple-element.13, f32[2048]{0:T(1024)S(1)} %log_add_fusion.2), kind=kLoop, calls=%fused_computation.10 | loop fusion | flops 16773120 | bytes 33579008 | tf_op jit(solution)/shard_map/reduce_sum | solution.py:28
  127.0 11.4 psum.64
  138.5 262.8 %all-reduce.4.cloned.1.call-done = f32[4096,1024]{1,0:T(8,128)} async-done(((f32[4096,1024]{1,0:T(8,128)}), f32[4096,1024]{1,0:T(8,128)}) %all-reduce.4.cloned.1.call-update) | async-done | bytes 16777232 | tf_op jit(solution)/shard_map/psum | solution.py:30
  401.3 7.0 multiply_reduce_fusion.1
  408.4 30.8 %fusion.21 = (f32[2048]{0:T(1024)S(1)}, f32[4096,2048]{1,0:T(8,128)}) fusion(f32[4096]{0:T(1024)S(1)} %multiply_reduce_fusion.1, bf16[2048,1024]{1,0:T(8,128)(2,1)} %param.4, f32[4096,1024]{1,0:T(8,128)} %all-reduce.4.cloned.1.call-done, f32[4096]{0:T(1024)S(1)} %get-tuple-element.7, f32[2048]{0:T(1024)S(1)} %fusion.15, f32[]{:T(128)} %bitcast.1, ...), kind=kOutput, calls=%fused_computation.43 | convolution fusion | flops 17238587392 | bytes 54591492 | tf_op jit(solution)/shard_map/nd,kd->nk/dot_general | solution.py:22
  439.1 11.8 pmax.22
  451.0 13.3 %exponential_reduce_fusion.1 = f32[2048]{0:T(1024)S(1)} fusion(f32[4096,2048]{1,0:T(8,128)} %get-tuple-element.15, f32[2048]{0:T(1024)S(1)} %pmax.22), kind=kLoop, calls=%fused_computation.1 | loop fusion | flops 16775168 | bytes 33570816 | tf_op jit(solution)/shard_map/reduce_sum | solution.py:25
  464.3 8.7 psum.66
  473.0 26.1 %fusion.8 = f32[4096,1024]{1,0:T(8,128)} fusion(bf16[2048,1024]{1,0:T(8,128)(2,1)} %param.4, f32[4096,2048]{1,0:T(8,128)} %get-tuple-element.15, f32[2048]{0:T(1024)S(1)} %log_add_fusion.1), kind=kOutput, calls=%fused_computation.16 | convolution fusion | flops 17196646400 | bytes 54534144 | tf_op jit(solution)/shard_map/nk,nd->kd/dot_general | solution.py:29
  499.1 0.0 all-reduce.6.cloned.1.call-update
  499.1 0.0 all-reduce.8.cloned.1.call-start
  499.2 13.3 %fusion.2 = f32[4096]{0:T(1024)S(1)} fusion(f32[4096,2048]{1,0:T(8,128)} %get-tuple-element.15, f32[2048]{0:T(1024)S(1)} %log_add_fusion.1), kind=kLoop, calls=%fused_computation.11 | loop fusion | flops 16773120 | bytes 33579008 | tf_op jit(solution)/shard_map/reduce_sum | solution.py:28
  512.5 11.6 psum.67
  524.1 262.3 %all-reduce.6.cloned.1.call-done = f32[4096,1024]{1,0:T(8,128)} async-done(((f32[4096,1024]{1,0:T(8,128)}), f32[4096,1024]{1,0:T(8,128)}) %all-reduce.6.cloned.1.call-update) | async-done | bytes 16777232 | tf_op jit(solution)/shard_map/psum | solution.py:30
  786.4 7.0 multiply_reduce_fusion
  793.4 30.8 %fusion.22 = (f32[2048]{0:T(1024)S(1)}, f32[4096,2048]{1,0:T(8,128)}) fusion(f32[4096]{0:T(1024)S(1)} %multiply_reduce_fusion, bf16[2048,1024]{1,0:T(8,128)(2,1)} %param.4, f32[4096,1024]{1,0:T(8,128)} %all-reduce.6.cloned.1.call-done, f32[4096]{0:T(1024)S(1)} %get-tuple-element.5, f32[2048]{0:T(1024)S(1)} %fusion.15, f32[]{:T(128)} %bitcast.2, ...), kind=kOutput, calls=%fused_computation.44 | convolution fusion | flops 17238587392 | bytes 54591492 | tf_op jit(solution)/shard_map/nd,kd->nk/dot_general | solution.py:22
  824.2 11.8 pmax.23
  836.0 13.3 %exponential_reduce_fusion = f32[2048]{0:T(1024)S(1)} fusion(f32[4096,2048]{1,0:T(8,128)} %get-tuple-element.17, f32[2048]{0:T(1024)S(1)} %pmax.23), kind=kLoop, calls=%fused_computation | loop fusion | flops 16775168 | bytes 33570816 | tf_op jit(solution)/shard_map/reduce_sum | solution.py:25
  849.3 8.8 psum.69
  858.1 0.0 copy-start
  858.1 26.1 %fusion.6 = f32[4096,1024]{1,0:T(8,128)} fusion(bf16[2048,1024]{1,0:T(8,128)(2,1)} %param.4, f32[4096,2048]{1,0:T(8,128)} %get-tuple-element.17, f32[2048]{0:T(1024)S(1)} %log_add_fusion), kind=kOutput, calls=%fused_computation.15 | convolution fusion | flops 17196646400 | bytes 54534144 | tf_op jit(solution)/shard_map/nk,nd->kd/dot_general | solution.py:29
  884.2 0.0 all-reduce.8.cloned.1.call-update
  884.2 0.0 copy-done
  884.3 13.3 %fusion.4 = f32[4096]{0:T(1024)S(1)} fusion(f32[4096,2048]{1,0:T(8,128)} %get-tuple-element.17, f32[2048]{0:T(1024)S(1)} %log_add_fusion), kind=kLoop, calls=%fused_computation.13 | loop fusion | flops 16773120 | bytes 33579008 | tf_op jit(solution)/shard_map/reduce_sum | solution.py:28
  897.6 11.3 psum.71
  908.9 0.6 multiply_log_fusion
  909.5 262.0 %all-reduce.8.cloned.1.call-done = f32[4096,1024]{1,0:T(8,128)} async-done(((f32[4096,1024]{1,0:T(8,128)}), f32[4096,1024]{1,0:T(8,128)}) %all-reduce.8.cloned.1.call-update) | async-done | bytes 16777232 | tf_op jit(solution)/shard_map/psum | solution.py:30
  1171.5 11.8 broadcast_divide_fusion
  (5 shorter events, 0.0 us)
Async XLA Ops:
  7.2 394.2 %all-reduce.4.cloned.1.call-start = ((), (), s32[]{:S(2)}) async-start(), calls=%async_computation | async-start | bytes 33554432 | tf_op jit(solution)/shard_map/psum | solution.py:30
  113.2 673.2 %all-reduce.6.cloned.1.call-start = ((), (), s32[]{:S(2)}) async-start(), calls=%async_computation.1 | async-start | bytes 33554432 | tf_op jit(solution)/shard_map/psum | solution.py:30
  499.1 672.4 %all-reduce.8.cloned.1.call-start = ((), (), s32[]{:S(2)}) async-start(), calls=%async_computation.2 | async-start | bytes 33554432 | tf_op jit(solution)/shard_map/psum | solution.py:30
  858.1 26.1 %copy-start = (f32[2048]{0:T(1024)}, f32[2048]{0:T(1024)S(1)}, u32[]{:S(2)}) copy-start(f32[2048]{0:T(1024)S(1)} %log_add_fusion) | copy-start | bytes 24580
Sparse Core Ops, SparseCore 0:
  113.3 287.9 all-reduce.3
  499.2 287.0 all-reduce.5
  884.4 287.1 all-reduce.7
where the time goes:
time: 1200 us; the launch traced here: 1190 us
  waiting for transfers between devices  787 us (66%)
  matrix products  172 us (14%)
  other arithmetic  117 us (10%)
  blocking collectives  98.2 us (8%)
  between operations  14.4 us (1%)
    psum x3, waiting for transfers between devices, per_device(): counts, stat_sums = lax.psum((counts, stat_sums), 'pts')  787 us
    dot_general x3, matrix products, per_device(): jnp.einsum('nd,kd->nk', points, mean_bf, preferred_element_type=jnp.float32)  92.7 us
    dot_general x3, matrix products, per_device(): jnp.einsum('nk,nd->kd', resp_prob.astype(jnp.bfloat16), points, preferred...  79.2 us
    reduce_sum x3, other arithmetic, per_device(): counts = jnp.sum(resp_prob, axis=0)  40.5 us
    reduce_sum x3, other arithmetic, per_device(): jnp.sum(jnp.exp(logits - row_top[:, None]), axis=1)  40.1 us
    pmax x3, blocking collectives, per_device(): row_top = lax.pmax(jnp.max(logits, axis=1), 'comp')  37.3 us
    psum x3, blocking collectives, per_device(): counts, stat_sums = lax.psum((counts, stat_sums), 'pts')  34.3 us
    psum x3, blocking collectives, per_device(): lax.psum(jnp.sum(jnp.exp(logits - row_top[:, None]), axis=1), 'comp')  26.6 us
  transfers between devices with their start and end apart: 3, of which 3 were waited for; matrix products, arithmetic and copies ran while one was open for 3% of the time, Pallas kernels for 0%

commit v1 on v0

v1 whole, which is shorter than its diff:
```python
import jax
import jax.numpy as jnp
from jax import lax
from jax.experimental import pallas as pl
from jax.experimental.pallas import tpu as pltpu
from jax.sharding import PartitionSpec as P

PRIOR_ALPHA = 1e-3
COUNT_EPS = 1e-6
F32, BF16 = jnp.float32, jnp.bfloat16
MESH = pl.DeviceIdType.MESH

NB = 1024
STRIP = NB // 2
PIECE = 128
CH = 256


def flip(p, a):
    y = lax.rem(p // 2 + a // 2, 2)
    c = lax.rem(lax.rem(p, 2) + lax.rem(a, 2), 2)
    return 2 * y + c


def em_kernel(beta, x_in, mu_in, lw_in, q_in, mu_out, n_out, lse_out, xg,
              pm, xbuf, mub, ab0, ab1, rb0, rb1, S, nacc, hmu_b, lw_b, mst, sst, qv, lse,
              own1, buf1, own2, buf2,
              fsem, xsem, qsend, qrecv, s1s, s1r, s2s, s2r,
              sib_s, sib_r, py_s, py_r, pz_s, pz_r, fw_s, fw_r, osem):
    kd, d = S.shape
    nblk = pm.shape[0]
    sweeps = beta.shape[0]
    z, p = lax.axis_index("comp"), lax.axis_index("pts")
    half = lax.rem(z, 2)
    zpair = z + 1 - 2 * half
    p1, p2 = flip(p, 1), flip(p, 2)

    barrier = pltpu.get_barrier_semaphore()
    for a in (1, 2, 3):
        pl.semaphore_signal(barrier, inc=1, device_id={"comp": lax.rem(z + a, 4)}, device_id_type=MESH)
        pl.semaphore_signal(barrier, inc=1, device_id={"pts": flip(p, a)}, device_id_type=MESH)
    pl.semaphore_wait(barrier, 6)

    def remote(src, dst, ss, rs, **dev):
        return pltpu.make_async_remote_copy(src_ref=src, dst_ref=dst, send_sem=ss, recv_sem=rs, device_id=dev, device_id_type=MESH)

    def rows(o, hf, i):
        return pl.ds(pl.multiple_of(o * 2048 + hf * 1024 + i * PIECE, PIECE), PIECE)

    own_rows = pl.ds(pl.multiple_of(p * 2048, 2048), 2048)
    sib = remote(x_in, xg.at[own_rows], sib_s, sib_r, pts=p1)
    py = lambda i: remote(x_in.at[pl.ds(pl.multiple_of(half * 1024 + i * PIECE, PIECE), PIECE)], xg.at[rows(p, half, i)], py_s.at[i], py_r.at[i], pts=p2)
    pz = lambda i: remote(xg.at[rows(p2, half, i)], xg.at[rows(p2, half, i)], pz_s.at[i], pz_r.at[i], comp=zpair)
    fwa = lambda i: remote(xg.at[rows(p2, half, i)], xg.at[rows(p2, half, i)], fw_s.at[i], fw_r.at[i], pts=p1)
    fwb = lambda i: remote(xg.at[rows(p2, 1 - half, i)], xg.at[rows(p2, 1 - half, i)], fw_s.at[8 + i], fw_r.at[8 + i], pts=p1)
    for i in range(8):
        py(i).start()
    qrow = lambda o: pl.ds(2 * o, 2)
    qcp = [remote(q_in, qv.at[qrow(p)], qsend.at[a - 1], qrecv.at[a - 1], pts=flip(p, a)) for a in (1, 2, 3)]
    for c in qcp:
        c.start()
    sib.start()
    st = [pltpu.make_async_copy(x_in.at[pl.ds(i * 1024, 1024)], (rb0, rb1)[i], xsem.at[i]) for i in range(2)]
    for c in st:
        c.start()
    mcp = pltpu.make_async_copy(mu_in.at[pl.ds(pl.multiple_of(p * kd, kd), kd)], S, osem)
    mcp.start()
    qv[qrow(p)] = q_in[...]
    lw_b[...] = lw_in[...]
    for i, c in enumerate(st):
        c.wait()
        st[i] = pltpu.make_async_copy((rb0, rb1)[i], xg.at[pl.ds(pl.multiple_of(p * 2048 + i * 1024, 1024), 1024)], xsem.at[i])
        st[i].start()
    mcp.wait()
    for c in st:
        c.wait()
    for c in qcp:
        c.wait()

    def take_py(i):
        py(i).wait_recv()
        pz(i).start()
        fwa(i).start()

    def take_pz(i):
        pz(i).wait_recv()
        fwb(i).start()

    def arrive(n):
        if n == 2:
            sib.wait_recv()
        elif n == 4:
            take_py(0)
            for i in range(1, 5):
                take_py(i)
                take_pz(i - 1)
        elif n == 6:
            for i in range(5, 8):
                take_py(i)
                take_pz(i - 1)
            take_pz(7)
        elif n in (5, 7):
            for i in range(4):
                fwa(i + 4 * (n == 7)).wait_recv()
                fwb(i + 4 * (n == 7)).wait_recv()

    def fetch(b, slot):
        o, h = b // 2, lax.rem(b, 2)
        return [pltpu.make_async_copy(xg.at[pl.ds(pl.multiple_of(o * 2048 + g * 1024 + h * STRIP, STRIP), STRIP)],
                                      xbuf.at[slot, pl.ds(g * STRIP, STRIP)], fsem.at[slot, g]) for g in range(2)]

    def start(cs):
        for c in cs:
            c.start()

    def wait(cs):
        for c in cs:
            c.wait()

    def sweep(t, _):
        par = lax.rem(t, 2)
        first_sweep = t == 0
        pe = jnp.where(first_sweep, p, 0)
        nb2 = -2.0 * beta[t]

        def order(k):
            r = 2 * (k // 4) + jnp.where(first_sweep, lax.rem(k, 2) * (k // 4) + (lax.rem(k, 4) // 2) * (1 - k // 4), lax.rem(k, 4) // 2)
            h = jnp.where(first_sweep, lax.rem(k, 2) * (1 - k // 4) + (lax.rem(k, 4) // 2) * (k // 4), lax.rem(k, 2))
            return 2 * flip(pe, r) + h

        start(fetch(order(0), 0))
        mub[...] = S[...].astype(BF16)
        hmu_b[...] = jnp.broadcast_to(0.5 * jnp.sum(S[...] * S[...], axis=1, keepdims=True), hmu_b.shape)
        nacc[...] = jnp.zeros_like(nacc)

        def send1(k):
            return [remote(own1.at[k], buf1.at[a - 1, k], s1s.at[a - 1, k], s1r.at[a - 1, k], comp=lax.rem(z + a, 4)) for a in (1, 2, 3)]

        def send2(b):
            return [remote(own2.at[b], buf2.at[par, a - 1, b], s2s.at[a - 1, b], s2r.at[par, a - 1, b], pts=flip(p, a)) for a in (1, 2, 3)]

        def merge(ms):
            m, s = [v[0:1] for v in ms], [v[1:2] for v in ms]
            top = jnp.maximum(jnp.maximum(m[0], m[1]), jnp.maximum(m[2], m[3]))
            return top, sum(si * jnp.exp(mi - top) for mi, si in zip(m, s))

        def publish(k):
            b = order(k)
            mm = jnp.max(mst[b], axis=0, keepdims=True)
            own1[k, 0:1] = mm
            own1[k, 1:2] = jnp.sum(sst[b] * jnp.exp(mst[b] - mm), axis=0, keepdims=True)
            start(send1(k))

        def relay(k):
            wait(send1(k))
            b = order(k)
            mm, ss = merge([own1[k]] + [buf1[a, k] for a in range(3)])
            own2[b, 0:1] = mm
            own2[b, 1:2] = ss
            start(send2(b))

        def settle(b):
            wait(send2(b))
            mm, ss = merge([own2[b]] + [buf2[par, a, b] for a in range(3)])
            l = mm + jnp.log(ss)
            lse[b] = l
            mst[b] = jnp.exp(mst[b] - l)

        def step_a(k, dst, src, slot, first, last, prepare):
            if not last:
                wait(fetch(order(k), slot))
                for cond, n in prepare:
                    @pl.when(jnp.logical_and(first_sweep, cond))
                    def _():
                        arrive(n)
                if prepare:
                    start(fetch(order(k + 1), 1 - slot))
            if not first:
                b = order(k - 1)
            for u in range(NB // 256):
                sl = slice(u * 256, (u + 1) * 256)
                if not last:
                    dst[:, sl] = lax.dot_general(mub[...], xbuf[slot, sl, :], (((1,), (1,)), ((), ())), preferred_element_type=F32)
                if not first:
                    for l0 in (u * 256, u * 256 + 128):
                        ln = slice(l0, l0 + 128)
                        q = jnp.broadcast_to(qv[b, :, ln], (CH, 128))
                        for c in range(kd // CH):
                            r = slice(c * CH, (c + 1) * CH)
                            lg = lw_b[r, :] + nb2 * ((hmu_b[r, :] - src[r, ln]) + q)
                            m = jnp.max(lg, axis=0, keepdims=True)
                            e = jnp.exp(lg - m)
                            pm[b, r, ln] = e
                            mst[b, c:c + 1, ln] = m
                            sst[b, c:c + 1, ln] = jnp.sum(e, axis=0, keepdims=True)
            if not first:
                publish(k - 1)

        yes = t >= 0
        step_a(0, ab0, ab1, 0, True, False, [(yes, 1)])

        def body_a(i, _):
            step_a(2 * i + 1, ab1, ab0, 1, False, False, [(i == 0, 2), (i == 1, 4), (i == 2, 6)])

            @pl.when(i > 0)
            def _():
                relay(2 * i - 2)
                relay(2 * i - 1)
            step_a(2 * i + 2, ab0, ab1, 0, False, False, [(i == 1, 5), (i == 2, 7)])
            return 0

        lax.fori_loop(0, nblk // 2 - 1, body_a, 0)
        step_a(nblk - 1, ab1, ab0, 1, False, False, [])
        start(fetch(0, 0))
        relay(nblk - 4)
        relay(nblk - 3)
        step_a(nblk, ab0, ab1, 0, False, True, [])
        relay(nblk - 2)
        relay(nblk - 1)

        S[...] = jnp.zeros_like(S)

        def step_s(j, rd, rs, slot, first, last):
            if not last:
                settle(j)
            if not first:
                wait(fetch(j - 1, slot))
                if not last:
                    start(fetch(j, 1 - slot))
            for u in range(4):
                if not last:
                    for r0 in range(u * (kd // 4), (u + 1) * (kd // 4), 16):
                        r = slice(r0, r0 + 16)
                        c = r0 // CH
                        rr = pm[j, r, :] * jnp.broadcast_to(mst[j, c:c + 1, :], (16, NB))
                        rd[r, :] = rr.astype(BF16)
                        acc = rr[:, 0:128]
                        for l0 in range(128, NB, 128):
                            acc += rr[:, l0:l0 + 128]
                        nacc[r, :] += acc
                if not first:
                    sl = slice(u * (d // 4), (u + 1) * (d // 4))
                    S[:, sl] += jnp.dot(rs[...], xbuf[slot, :, sl], preferred_element_type=F32)

        step_s(0, rb0, rb1, 1, True, False)

        def body_s(i, _):
            step_s(2 * i + 1, rb1, rb0, 0, False, False)
            step_s(2 * i + 2, rb0, rb1, 1, False, False)
            return 0

        lax.fori_loop(0, nblk // 2 - 1, body_s, 0)
        step_s(nblk - 1, rb1, rb0, 0, False, False)
        step_s(nblk, rb0, rb1, 1, False, True)
        n = jnp.sum(nacc[...], axis=1, keepdims=True)
        S[...] = S[...] * (1.0 / (n + COUNT_EPS))
        lw = jnp.log((n + PRIOR_ALPHA) / (nblk * NB + 16 * kd * PRIOR_ALPHA))
        lw_b[...] = jnp.broadcast_to(lw, lw_b.shape)
        return 0

    lax.fori_loop(0, sweeps, sweep, 0)

    sib.wait_send()
    for i in range(8):
        py(i).wait_send()
        pz(i).wait_send()
        fwa(i).wait_send()
        fwb(i).wait_send()
    ocp = pltpu.make_async_copy(S, mu_out, osem)
    ocp.start()
    n_out[...] = lw_b[...]
    lse_out[...] = lse[qrow(p)]
    ocp.wait()


def solution(mesh):
    def per_device(points, mean_vecs, log_w, inv_temp):
        n_loc, d = points.shape
        k_loc = mean_vecs.shape[0]
        kd = k_loc // mesh.shape["pts"]
        nblk = n_loc * mesh.shape["pts"] // NB
        p = lax.axis_index("pts")
        x_sq = 0.5 * jnp.sum(jnp.square(points.astype(F32)), axis=1)
        q_in = x_sq.reshape(2, 2, STRIP).transpose(1, 0, 2).reshape(2, 1, NB)
        lw_in = jnp.broadcast_to(lax.dynamic_slice(log_w, (p * kd,), (kd,))[:, None], (kd, 128))
        V, D = pltpu.VMEM, pltpu.SemaphoreType.DMA
        bs = lambda m: pl.BlockSpec(memory_space=m)
        mu, lw_b, lse, _ = pl.pallas_call(
            em_kernel,
            out_shape=(
                jax.ShapeDtypeStruct((kd, d), F32),
                jax.ShapeDtypeStruct((kd, 128), F32),
                jax.ShapeDtypeStruct((2, 1, NB), F32),
                jax.ShapeDtypeStruct((nblk * NB, d), BF16),
            ),
            in_specs=[bs(pltpu.SMEM), bs(pl.ANY), bs(pl.ANY), bs(V), bs(V)],
            out_specs=(bs(pl.ANY), bs(V), bs(V), bs(pl.ANY)),
            scratch_shapes=[
                V((nblk, kd, NB), F32), V((2, NB, d), BF16), V((kd, d), BF16),
                V((kd, NB), F32), V((kd, NB), F32), V((kd, NB), BF16), V((kd, NB), BF16),
                V((kd, d), F32), V((kd, 128), F32), V((kd, 128), F32), V((kd, 128), F32),
                V((nblk, kd // CH, NB), F32), V((nblk, kd // CH, NB), F32),
                V((nblk, 1, NB), F32), V((nblk, 1, NB), F32),
                V((nblk, 2, NB), F32), V((3, nblk, 2, NB), F32),
                V((nblk, 2, NB), F32), V((2, 3, nblk, 2, NB), F32),
                D((2, 2)), D((2,)), D((3,)), D((3,)),
                D((3, nblk)), D((3, nblk)), D((3, nblk)), D((2, 3, nblk)),
                D, D, D((8,)), D((8,)), D((8,)), D((8,)), D((16,)), D((16,)), D,
            ],
            compiler_params=pltpu.CompilerParams(
                collective_id=0, has_side_effects=True, vmem_limit_bytes=67043328),
            name="em_sweeps",
        )(inv_temp, points, mean_vecs, lw_in, q_in)
        means = lax.all_gather(mu, "pts", axis=0, tiled=True)
        logw = lax.all_gather(lw_b[:, 0], "pts", axis=0, tiled=True)
        lse_rows = lse.reshape(2, 2, STRIP).transpose(1, 0, 2).reshape(n_loc)
        return means, logw, lse_rows

    comp_spec, row_spec = P(("fit", "comp")), P(("fit", "pts"))
    return jax.shard_map(
        per_device,
        mesh=mesh,
        in_specs=(P(("fit", "pts"), None), P(("fit", "comp"), None), comp_spec, P()),
        out_specs=(P(("fit", "comp"), None), comp_spec, row_spec),
        check_vma=False,
    )
```

time: 1200 us -> 414 us (0.34)
  waiting for transfers between devices: 787 us -> 87.6 us
  Pallas kernels: 0 us -> 275 us
  matrix products: 172 us -> 0 us
  other arithmetic: 117 us -> 5.03 us
  blocking collectives: 98.2 us -> 17 us
  local copies, waits for them, and re-layouts: 1.39 us -> 14.9 us
    psum x3 -> x0, waiting for transfers between devices: 787 us -> none  [per_device(): counts, stat_sums = lax.psum((counts, stat_sums), 'pts')]
    pallas_call x0 -> x1, Pallas kernels: none -> 275 us  [per_device(): pl.pallas_call(em_kernel, out_shape=(jax.ShapeDtypeStruct((kd, d), F32),...]
    dot_general x6 -> x0, matrix products: 172 us -> none  [the longest x3 92.7 us: per_device(): jnp.einsum('nd,kd->nk', points, mean_bf, preferred_element_type=jnp.float32)]
    reduce_sum x9 -> x1, other arithmetic: 102 us -> 3.08 us  [per_device(): x_sq = 0.5 * jnp.sum(jnp.square(points.astype(F32)), axis=1)]
    all_gather x0 -> x1, waiting for transfers between devices: none -> 87.5 us  [per_device(): means = lax.all_gather(mu, 'pts', axis=0, tiled=True)]
    psum x6 -> x0, blocking collectives: 60.9 us -> none  [the longest x3 34.3 us: per_device(): counts, stat_sums = lax.psum((counts, stat_sums), 'pts')]
    pmax x3 -> x0, blocking collectives: 37.3 us -> none  [per_device(): row_top = lax.pmax(jnp.max(logits, axis=1), 'comp')]
    all_gather x0 -> x1, blocking collectives: none -> 17 us  [per_device(): logw = lax.all_gather(lw_b[:, 0], 'pts', axis=0, tiled=True)]
  transfers between devices with their start and end apart: 3 -> 1, of which waited for: 3 -> 1; matrix products, arithmetic and copies ran while one was open for 3% -> 1% of each run, Pallas kernels for 0% -> 0%
where the time goes in v1:
time: 414 us; the launch traced here: 413 us
  Pallas kernels  275 us (66%)
  waiting for transfers between devices  87.6 us (21%)
  blocking collectives  17 us (4%)
  local copies, waits for them, and re-layouts  14.9 us (4%)
  between operations  14.1 us (3%)
  other arithmetic  5.03 us (1%)
    pallas_call x1, Pallas kernels, per_device(): pl.pallas_call(em_kernel, out_shape=(jax.ShapeDtypeStruct((kd, d), F32),...  275 us
    all_gather x1, waiting for transfers between devices, per_device(): means = lax.all_gather(mu, 'pts', axis=0, tiled=True)  87.5 us
    all_gather x1, blocking collectives, per_device(): logw = lax.all_gather(lw_b[:, 0], 'pts', axis=0, tiled=True)  17 us
    unnamed x2, local copies, waits for them, and re-layouts  12.6 us
  transfers between devices with their start and end apart: 1, of which 1 were waited for; matrix products, arithmetic and copies ran while one was open for 1% of the time, Pallas kernels for 0%

profile of v1, /device:TPU:0, one launch (start us, length us, event | category | flops | bytes accessed | tf_op | source)
XLA Modules:
  0.0 413.3 jit_solution(1761113351099555819)
XLA Ops:
  7.2 0.0 all-gather.3.cloned.1.call-start
  7.2 3.1 multiply_reduce_fusion
  10.3 0.6 reshape.20.q_in
  11.0 0.7 dynamic_slice.3
  11.6 1.0 broadcast_in_dim.2.lw_in
  12.6 274.7 %em_sweeps.1 = (f32[1024,1024]{1,0:T(8,128)}, f32[1024,128]{1,0:T(8,128)}, f32[2,1,1024]{2,1,0:T(1,128)}, bf16[8192,1024]{1,0:T(8,128)(2,1)}) custom-call(f32[3]{0:T(128)} %beta.1, bf16[2048,1024]{1,0:T(8,128)(2,1)} %x_in.1, f32[4096,1024]{1,0:T(8,128)} %mu_in.1, f32[1024,128]{1,0:T(8,128)} %broadcast_in_dim.2.lw_in, f32[2,1,1024]{2,1,0:T(1,128)} %reshape.20.q_in), custom_call_target="tpu_custom_call" | custom-call | tf_op jit(solution)/shard_map/em_sweeps/pallas_call | solution.py:288
  287.4 0.0 all-gather.3.cloned.1.call-update
  287.4 0.7 reduce.1
  288.1 0.6 copy.9
  288.7 17.0 %all-gather = f32[4096,1]{1,0:T(8,128)S(1)} all-gather(f32[1024,1]{1,0:T(8,128)} %bitcast.7), channel_id=2, replica_groups=mesh['fit'=2,'comp'=4,'pts'=4] {'pts'}, dimensions={0}, use_global_device_ids=true | all-gather | bytes 20480 | tf_op jit(solution)/shard_map/all_gather | solution.py:315
  305.7 1.2 reduce
  306.9 87.5 %all-gather.3.cloned.1.call-done = f32[4096,1024]{1,0:T(8,128)} async-done(((f32[1024,1024]{1,0:T(8,128)}), f32[4096,1024]{1,0:T(8,128)}) %all-gather.3.cloned.1.call-update) | async-done | bytes 16777232 | tf_op jit(solution)/shard_map/all_gather | solution.py:314
  394.5 12.0 %copy.11 = f32[4096,1024]{1,0:T(8,128)} copy(f32[4096,1024]{1,0:T(8,128)} %all-gather.3.cloned.1.call-done) | data formatting | bytes 33554432
  (3 shorter events, 0.0 us)
Async XLA Ops:
  7.2 387.3 %all-gather.3.cloned.1.call-start = ((), (), s32[]{:S(2)}) async-start(), calls=%async_computation | async-start | bytes 20971520 | tf_op jit(solution)/shard_map/all_gather | solution.py:314
Sparse Core Ops, SparseCore 0:
  287.5 106.9 all-gather.2

commit v2 on v1

--- a/solution.py
+++ b/solution.py
@@ -13,6 +13,7 @@
 NB = 1024
 STRIP = NB // 2
 PIECE = 128
+FAR = 384
 CH = 256
 
 
@@ -22,11 +23,12 @@
     return 2 * y + c
 
 
-def em_kernel(beta, x_in, mu_in, lw_in, q_in, mu_out, n_out, lse_out, xg,
+def em_kernel(beta, x_in, mu_in, lw_in, q_in, mu_out, lw_out, lse_out, xg,
               pm, xbuf, mub, ab0, ab1, rb0, rb1, S, nacc, hmu_b, lw_b, mst, sst, qv, lse,
-              own1, buf1, own2, buf2,
+              own1, buf1, own2, buf2, mub2, hmu_b2, lw_b2, row1, row2, lw_all,
               fsem, xsem, qsend, qrecv, s1s, s1r, s2s, s2r,
-              sib_s, sib_r, py_s, py_r, pz_s, pz_r, fw_s, fw_r, osem):
+              sib_s, sib_r, py_s, py_r, pz_s, pz_r, fw_s, fw_r,
+              b_s, b_r, w_s, w_r, o_s, o_r, osem):
     kd, d = S.shape
     nblk = pm.shape[0]
     sweeps = beta.shape[0]
@@ -53,29 +55,41 @@
     pz = lambda i: remote(xg.at[rows(p2, half, i)], xg.at[rows(p2, half, i)], pz_s.at[i], pz_r.at[i], comp=zpair)
     fwa = lambda i: remote(xg.at[rows(p2, half, i)], xg.at[rows(p2, half, i)], fw_s.at[i], fw_r.at[i], pts=p1)
     fwb = lambda i: remote(xg.at[rows(p2, 1 - half, i)], xg.at[rows(p2, 1 - half, i)], fw_s.at[8 + i], fw_r.at[8 + i], pts=p1)
-    for i in range(8):
-        py(i).start()
     qrow = lambda o: pl.ds(2 * o, 2)
     qcp = [remote(q_in, qv.at[qrow(p)], qsend.at[a - 1], qrecv.at[a - 1], pts=flip(p, a)) for a in (1, 2, 3)]
     for c in qcp:
         c.start()
+    for i in range(8):
+        py(i).start()
     sib.start()
     st = [pltpu.make_async_copy(x_in.at[pl.ds(i * 1024, 1024)], (rb0, rb1)[i], xsem.at[i]) for i in range(2)]
     for c in st:
         c.start()
-    mcp = pltpu.make_async_copy(mu_in.at[pl.ds(pl.multiple_of(p * kd, kd), kd)], S, osem)
+    mcp = pltpu.make_async_copy(mu_in.at[pl.ds(pl.multiple_of(p * kd, kd), kd)], S, osem.at[0])
     mcp.start()
+    lcp = pltpu.make_async_copy(lw_in, lw_b, osem.at[1])
+    lcp.start()
     qv[qrow(p)] = q_in[...]
-    lw_b[...] = lw_in[...]
     for i, c in enumerate(st):
         c.wait()
         st[i] = pltpu.make_async_copy((rb0, rb1)[i], xg.at[pl.ds(pl.multiple_of(p * 2048 + i * 1024, 1024), 1024)], xsem.at[i])
         st[i].start()
     mcp.wait()
+    lcp.wait()
     for c in st:
         c.wait()
     for c in qcp:
         c.wait()
+
+    rest = pl.ds(FAR, kd - FAR)
+    mid = (kd - FAR) // 2
+    bulk = lambda i: remote(mub.at[pl.ds(FAR + i * mid, mid)], mub2.at[pl.ds(i * mid, mid)], b_s.at[i], b_r.at[i], pts=p2)
+    bulk_rows = lambda: remote(row1, row2, b_s.at[2], b_r.at[2], pts=p2)
+
+    def as_row(ref, g):
+        blk = ref[g * 128:(g + 1) * 128, :]
+        eye = lax.broadcasted_iota(jnp.int32, (128, 128), 0) == lax.broadcasted_iota(jnp.int32, (128, 128), 1)
+        return jnp.sum(jnp.where(eye, blk, 0.0), axis=0, keepdims=True)
 
     def take_py(i):
         py(i).wait_recv()
@@ -129,9 +143,23 @@
             return 2 * flip(pe, r) + h
 
         start(fetch(order(0), 0))
-        mub[...] = S[...].astype(BF16)
-        hmu_b[...] = jnp.broadcast_to(0.5 * jnp.sum(S[...] * S[...], axis=1, keepdims=True), hmu_b.shape)
-        nacc[...] = jnp.zeros_like(nacc)
+        def load_means(g, _):
+            r = pl.ds(pl.multiple_of(g * 64, 64), 64)
+            v = S[r, :]
+            mub[r, :] = v.astype(BF16)
+            hmu_b[r, :] = jnp.broadcast_to(0.5 * jnp.sum(v * v, axis=1, keepdims=True), (64, 128))
+            nacc[r, :] = jnp.zeros((64, 128), F32)
+            return 0
+
+        lax.fori_loop(0, kd // 64, load_means, 0)
+
+        @pl.when(t == sweeps - 1)
+        def _():
+            for g in range(kd // 128):
+                row1[0, g:g + 1, :] = as_row(hmu_b, g)
+                row1[1, g:g + 1, :] = as_row(lw_b, g)
+            bulk_rows().start()
+            bulk(0).start()
 
         def send1(k):
             return [remote(own1.at[k], buf1.at[a - 1, k], s1s.at[a - 1, k], s1r.at[a - 1, k], comp=lax.rem(z + a, 4)) for a in (1, 2, 3)]
@@ -216,7 +244,10 @@
         relay(nblk - 3)
         step_a(nblk, ab0, ab1, 0, False, True, [])
         relay(nblk - 2)
-        relay(nblk - 1)
+
+        @pl.when(first_sweep)
+        def _():
+            relay(nblk - 1)
 
         S[...] = jnp.zeros_like(S)
 
@@ -246,31 +277,128 @@
 
         def body_s(i, _):
             step_s(2 * i + 1, rb1, rb0, 0, False, False)
+
+            @pl.when(jnp.logical_and(i == 0, t > 0))
+            def _():
+                relay(nblk - 1)
+
+            @pl.when(jnp.logical_and(i == 0, t == sweeps - 1))
+            def _():
+                bulk(1).start()
             step_s(2 * i + 2, rb0, rb1, 1, False, False)
             return 0
 
         lax.fori_loop(0, nblk // 2 - 1, body_s, 0)
         step_s(nblk - 1, rb1, rb0, 0, False, False)
         step_s(nblk, rb0, rb1, 1, False, True)
-        n = jnp.sum(nacc[...], axis=1, keepdims=True)
-        S[...] = S[...] * (1.0 / (n + COUNT_EPS))
-        lw = jnp.log((n + PRIOR_ALPHA) / (nblk * NB + 16 * kd * PRIOR_ALPHA))
-        lw_b[...] = jnp.broadcast_to(lw, lw_b.shape)
+        def finish(g, _):
+            r = pl.ds(pl.multiple_of(g * 64, 64), 64)
+            n = jnp.sum(nacc[r, :], axis=1, keepdims=True)
+            S[r, :] = S[r, :] * (1.0 / (n + COUNT_EPS))
+            lw = jnp.log((n + PRIOR_ALPHA) / (nblk * NB + 16 * kd * PRIOR_ALPHA))
+            lw_b[r, :] = jnp.broadcast_to(lw, (64, 128))
+            return 0
+
+        lax.fori_loop(0, kd // 64, finish, 0)
         return 0
 
     lax.fori_loop(0, sweeps, sweep, 0)
 
+    quarter = lambda o, r0, n: pl.ds(pl.multiple_of(o * kd + r0, 128), n)
+    out_own = pltpu.make_async_copy(S, mu_out.at[quarter(p, 0, kd)], osem.at[0])
+    out_sib = remote(S, mu_out.at[quarter(p, 0, kd)], o_s.at[0], o_r.at[0], pts=p1)
+    out_far = [remote(S.at[pl.ds(i * 128, 128)], mu_out.at[quarter(p, i * 128, 128)], o_s.at[1 + i], o_r.at[1 + i], pts=p2) for i in range(FAR // 128)]
+    out_fwd = [remote(mu_out.at[quarter(p2, i * 128, 128)], mu_out.at[quarter(p2, i * 128, 128)], o_s.at[4 + i], o_r.at[4 + i], pts=p1) for i in range(FAR // 128)]
+    for g in range(kd // 128):
+        lw_all[p, g:g + 1, :] = as_row(lw_b, g)
+    out_lw = [remote(lw_all.at[p], lw_all.at[p], w_s.at[a - 1], w_r.at[a - 1], pts=flip(p, a)) for a in (1, 2, 3)]
+    start(out_lw)
+    start(out_far)
+    out_own.start()
+    out_sib.start()
+
+    rn = kd - FAR
+    S2 = pm.at[0]
+    bulk_rows().wait()
+    for i in range(2):
+        bulk(i).wait()
+    for g in range(rn // 128):
+        for v, ref in ((0, hmu_b2), (1, lw_b2)):
+            ref[g * 128:(g + 1) * 128, :] = jnp.broadcast_to(row2[v, FAR // 128 + g:FAR // 128 + g + 1, :], (128, 128)).T
+    nb2 = -2.0 * beta[sweeps - 1]
+    nacc[...] = jnp.zeros_like(nacc)
+    S2[0:rn, :] = jnp.zeros((rn, d), F32)
+    start(fetch(0, 0))
+
+    def step_d(j, dst, src, rb, first, last):
+        now, before = lax.rem(j, 3), lax.rem(j + 2, 3)
+        if not last:
+            wait(fetch(j, now))
+
+            @pl.when(j + 1 < nblk)
+            def _():
+                start(fetch(j + 1, lax.rem(j + 1, 3)))
+        for u in range(4):
+            if not last:
+                sl = slice(u * (NB // 4), (u + 1) * (NB // 4))
+                dst[0:rn, sl] = lax.dot_general(mub2[...], xbuf[now, sl, :], (((1,), (1,)), ((), ())), preferred_element_type=F32)
+            if not first:
+                for r0 in range(u * (rn // 4), (u + 1) * (rn // 4), 16):
+                    r = slice(r0, r0 + 16)
+                    wide = lambda ref: jnp.concatenate([ref[r, :]] * (NB // 128), axis=1)
+                    spread = lambda v: jnp.broadcast_to(v, (16, NB))
+                    lg = wide(lw_b2) + nb2 * ((wide(hmu_b2) - src[r, :]) + spread(qv[j - 1]))
+                    rr = jnp.exp(lg - spread(lse[j - 1]))
+                    rb[r, :] = rr.astype(BF16)
+                    acc = rr[:, 0:128]
+                    for l0 in range(128, NB, 128):
+                        acc += rr[:, l0:l0 + 128]
+                    nacc[r, :] += acc
+        if not first:
+            for u in range(4):
+                sl = slice(u * (d // 4), (u + 1) * (d // 4))
+                S2[0:rn, sl] += jnp.dot(rb[0:rn, :], xbuf[before, :, sl], preferred_element_type=F32)
+
+    step_d(0, ab0, ab1, rb0, True, False)
+
+    def body_d(i, _):
+        step_d(2 * i + 1, ab1, ab0, rb0, False, False)
+        step_d(2 * i + 2, ab0, ab1, rb1, False, False)
+        return 0
+
+    lax.fori_loop(0, nblk // 2 - 1, body_d, 0)
+    step_d(nblk - 1, ab1, ab0, rb0, False, False)
+    step_d(nblk, ab0, ab1, rb1, False, True)
+
+    def finish2(g, _):
+        r = pl.ds(pl.multiple_of(g * 64, 64), 64)
+        n2 = jnp.sum(nacc[r, :], axis=1, keepdims=True)
+        S2[r, :] = S2[r, :] * (1.0 / (n2 + COUNT_EPS))
+        return 0
+
+    lax.fori_loop(0, rn // 64, finish2, 0)
+    src2 = S2.at[pl.ds(0, rn)]
+    out_dup = pltpu.make_async_copy(src2, mu_out.at[quarter(p2, FAR, rn)], osem.at[1])
+    out_dsib = remote(src2, mu_out.at[quarter(p2, FAR, rn)], o_s.at[7], o_r.at[7], pts=p1)
+    out_dsib.start()
+    out_dup.start()
+    for c, f in zip(out_far, out_fwd):
+        c.wait()
+        f.start()
     sib.wait_send()
     for i in range(8):
         py(i).wait_send()
         pz(i).wait_send()
         fwa(i).wait_send()
         fwb(i).wait_send()
-    ocp = pltpu.make_async_copy(S, mu_out, osem)
-    ocp.start()
-    n_out[...] = lw_b[...]
+    wait(out_lw)
+    lw_out[...] = lw_all[...]
     lse_out[...] = lse[qrow(p)]
-    ocp.wait()
+    out_own.wait()
+    out_sib.wait()
+    wait(out_fwd)
+    out_dup.wait()
+    out_dsib.wait()
 
 
 def solution(mesh):
@@ -285,36 +413,37 @@
         lw_in = jnp.broadcast_to(lax.dynamic_slice(log_w, (p * kd,), (kd,))[:, None], (kd, 128))
         V, D = pltpu.VMEM, pltpu.SemaphoreType.DMA
         bs = lambda m: pl.BlockSpec(memory_space=m)
-        mu, lw_b, lse, _ = pl.pallas_call(
+        means, logw, lse, _ = pl.pallas_call(
             em_kernel,
             out_shape=(
-                jax.ShapeDtypeStruct((kd, d), F32),
-                jax.ShapeDtypeStruct((kd, 128), F32),
+                jax.ShapeDtypeStruct((k_loc, d), F32),
+                jax.ShapeDtypeStruct((k_loc // kd, kd // 128, 128), F32),
                 jax.ShapeDtypeStruct((2, 1, NB), F32),
                 jax.ShapeDtypeStruct((nblk * NB, d), BF16),
             ),
-            in_specs=[bs(pltpu.SMEM), bs(pl.ANY), bs(pl.ANY), bs(V), bs(V)],
+            in_specs=[bs(pltpu.SMEM), bs(pl.ANY), bs(pl.ANY), bs(pl.ANY), bs(V)],
             out_specs=(bs(pl.ANY), bs(V), bs(V), bs(pl.ANY)),
             scratch_shapes=[
-                V((nblk, kd, NB), F32), V((2, NB, d), BF16), V((kd, d), BF16),
+                V((nblk, kd, NB), F32), V((3, NB, d), BF16), V((kd, d), BF16),
                 V((kd, NB), F32), V((kd, NB), F32), V((kd, NB), BF16), V((kd, NB), BF16),
                 V((kd, d), F32), V((kd, 128), F32), V((kd, 128), F32), V((kd, 128), F32),
                 V((nblk, kd // CH, NB), F32), V((nblk, kd // CH, NB), F32),
                 V((nblk, 1, NB), F32), V((nblk, 1, NB), F32),
                 V((nblk, 2, NB), F32), V((3, nblk, 2, NB), F32),
                 V((nblk, 2, NB), F32), V((2, 3, nblk, 2, NB), F32),
-                D((2, 2)), D((2,)), D((3,)), D((3,)),
+                V((kd - FAR, d), BF16), V((kd - FAR, 128), F32), V((kd - FAR, 128), F32),
+                V((2, kd // 128, 128), F32), V((2, kd // 128, 128), F32), V((k_loc // kd, kd // 128, 128), F32),
+                D((3, 2)), D((2,)), D((3,)), D((3,)),
                 D((3, nblk)), D((3, nblk)), D((3, nblk)), D((2, 3, nblk)),
-                D, D, D((8,)), D((8,)), D((8,)), D((8,)), D((16,)), D((16,)), D,
+                D, D, D((8,)), D((8,)), D((8,)), D((8,)), D((16,)), D((16,)),
+                D((3,)), D((3,)), D((3,)), D((3,)), D((8,)), D((8,)), D((2,)),
             ],
             compiler_params=pltpu.CompilerParams(
                 collective_id=0, has_side_effects=True, vmem_limit_bytes=67043328),
             name="em_sweeps",
         )(inv_temp, points, mean_vecs, lw_in, q_in)
-        means = lax.all_gather(mu, "pts", axis=0, tiled=True)
-        logw = lax.all_gather(lw_b[:, 0], "pts", axis=0, tiled=True)
         lse_rows = lse.reshape(2, 2, STRIP).transpose(1, 0, 2).reshape(n_loc)
-        return means, logw, lse_rows
+        return means, logw.reshape(k_loc), lse_rows
 
     comp_spec, row_spec = P(("fit", "comp")), P(("fit", "pts"))
     return jax.shard_map(

time: 414 us -> 286 us (0.69)
  waiting for transfers between devices: 87.6 us -> 0 us
  blocking collectives: 17 us -> 0 us
  between operations: 14.1 us -> 0.67 us
  Pallas kernels: 275 us -> 266 us
    all_gather x1 -> x0, waiting for transfers between devices: 87.5 us -> none  [per_device(): means = lax.all_gather(mu, 'pts', axis=0, tiled=True)]
    all_gather x1 -> x0, blocking collectives: 17 us -> none  [per_device(): logw = lax.all_gather(lw_b[:, 0], 'pts', axis=0, tiled=True)]
    pallas_call x1, Pallas kernels: 275 us -> 266 us  [per_device(): pl.pallas_call(em_kernel, out_shape=(jax.ShapeDtypeStruct((k_loc, d), F32...]
    unnamed x2 -> x5, local copies, waits for them, and re-layouts: 12.6 us -> 13.2 us
  transfers between devices with their start and end apart: 1 -> 0, of which waited for: 1 -> 0; matrix products, arithmetic and copies ran while one was open for 1% -> 0% of each run, Pallas kernels for 0% -> 0%
where the time goes in v2:
time: 286 us; the launch traced here: 285 us
  Pallas kernels  266 us (93%)
  local copies, waits for them, and re-layouts  15.5 us (5%)
  other arithmetic  3.81 us (1%)
    pallas_call x1, Pallas kernels, per_device(): pl.pallas_call(em_kernel, out_shape=(jax.ShapeDtypeStruct((k_loc, d), F32...  266 us
    unnamed x5, local copies, waits for them, and re-layouts  13.2 us

profile of v2, /device:TPU:0, one launch (start us, length us, event | category | flops | bytes accessed | tf_op | source)
XLA Modules:
  0.0 285.5 jit_solution(2413944358333273465)
XLA Ops:
  0.6 0.7 dynamic_slice.3
  1.3 3.1 %multiply_reduce_fusion = f32[2048]{0:T(1024)S(1)} fusion(bf16[2048,1024]{1,0:T(8,128)(2,1)} %x_in.1), kind=kLoop, calls=%fused_computation | loop fusion | flops 6289408 | bytes 4202496 | tf_op jit(solution)/shard_map/reduce_sum | solution.py:411
  4.4 0.6 reshape.23.q_in
  5.1 1.0 broadcast_in_dim.2.lw_in
  6.1 265.5 %em_sweeps.1 = (f32[4096,1024]{1,0:T(8,128)}, f32[4,8,128]{2,1,0:T(8,128)}, f32[2,1,1024]{2,1,0:T(1,128)}, bf16[8192,1024]{1,0:T(8,128)(2,1)}) custom-call(f32[3]{0:T(128)} %beta.1, bf16[2048,1024]{1,0:T(8,128)(2,1)} %x_in.1, f32[4096,1024]{1,0:T(8,128)} %mu_in.1, f32[1024,128]{1,0:T(8,128)} %broadcast_in_dim.2.lw_in, f32[2,1,1024]{2,1,0:T(1,128)} %reshape.23.q_in), custom_call_target="tpu_custom_call" | custom-call | tf_op jit(solution)/shard_map/em_sweeps/pallas_call | solution.py:416
  271.6 0.7 reduce
  272.3 0.6 copy.9
  272.9 0.0 copy-start
  272.9 12.0 %copy.12 = f32[4096,1024]{1,0:T(8,128)} copy(f32[4096,1024]{1,0:T(8,128)} %get-tuple-element.12) | data formatting | bytes 33554432
  284.9 0.0 copy-done
  284.9 0.6 copy.13
  (3 shorter events, 0.0 us)
Async XLA Ops:
  272.9 12.0 %copy-start = (f32[4,8,128]{2,1,0:T(8,128)S(1)}, f32[4,8,128]{2,1,0:T(8,128)}, u32[]{:S(2)}) copy-start(f32[4,8,128]{2,1,0:T(8,128)} %get-tuple-element.7) | copy-start | bytes 49156

commit v3 on v2

--- a/solution.py
+++ b/solution.py
@@ -13,7 +13,7 @@
 NB = 1024
 STRIP = NB // 2
 PIECE = 128
-FAR = 384
+FAR = 256
 CH = 256
 
 
@@ -101,7 +101,7 @@
         fwb(i).start()
 
     def arrive(n):
-        if n == 2:
+        if n == 1:
             sib.wait_recv()
         elif n == 4:
             take_py(0)
@@ -109,9 +109,8 @@
                 take_py(i)
                 take_pz(i - 1)
         elif n == 6:
-            for i in range(5, 8):
-                take_py(i)
-                take_pz(i - 1)
+            take_py(7)
+            take_pz(6)
             take_pz(7)
         elif n in (5, 7):
             for i in range(4):
@@ -137,9 +136,12 @@
         pe = jnp.where(first_sweep, p, 0)
         nb2 = -2.0 * beta[t]
 
+        def order_s(j):
+            return 2 * lax.rem(j, 4) + j // 4
+
         def order(k):
-            r = 2 * (k // 4) + jnp.where(first_sweep, lax.rem(k, 2) * (k // 4) + (lax.rem(k, 4) // 2) * (1 - k // 4), lax.rem(k, 4) // 2)
-            h = jnp.where(first_sweep, lax.rem(k, 2) * (1 - k // 4) + (lax.rem(k, 4) // 2) * (k // 4), lax.rem(k, 2))
+            r = jnp.where(first_sweep, 2 * (k // 4) + lax.rem(k, 2), lax.rem(k, 4))
+            h = jnp.where(first_sweep, lax.rem(k, 4) // 2, k // 4)
             return 2 * flip(pe, r) + h
 
         start(fetch(order(0), 0))
@@ -194,15 +196,15 @@
             lse[b] = l
             mst[b] = jnp.exp(mst[b] - l)
 
-        def step_a(k, dst, src, slot, first, last, prepare):
+        def step_a(k, dst, src, slot, first, last, prepare=(), nxt=None):
             if not last:
                 wait(fetch(order(k), slot))
                 for cond, n in prepare:
                     @pl.when(jnp.logical_and(first_sweep, cond))
                     def _():
                         arrive(n)
-                if prepare:
-                    start(fetch(order(k + 1), 1 - slot))
+                if nxt is not None:
+                    start(fetch(nxt, 1 - slot))
             if not first:
                 b = order(k - 1)
             for u in range(NB // 256):
@@ -224,38 +226,50 @@
             if not first:
                 publish(k - 1)
 
-        yes = t >= 0
-        step_a(0, ab0, ab1, 0, True, False, [(yes, 1)])
-
-        def body_a(i, _):
-            step_a(2 * i + 1, ab1, ab0, 1, False, False, [(i == 0, 2), (i == 1, 4), (i == 2, 6)])
-
-            @pl.when(i > 0)
+        def rounds_a(g, a0, na, s0):
+            @pl.when(g == 1)
             def _():
-                relay(2 * i - 2)
-                relay(2 * i - 1)
-            step_a(2 * i + 2, ab0, ab1, 0, False, False, [(i == 1, 5), (i == 2, 7)])
-            return 0
-
-        lax.fori_loop(0, nblk // 2 - 1, body_a, 0)
-        step_a(nblk - 1, ab1, ab0, 1, False, False, [])
-        start(fetch(0, 0))
-        relay(nblk - 4)
-        relay(nblk - 3)
-        step_a(nblk, ab0, ab1, 0, False, True, [])
-        relay(nblk - 2)
-
-        @pl.when(first_sweep)
-        def _():
-            relay(nblk - 1)
-
-        S[...] = jnp.zeros_like(S)
-
-        def step_s(j, rd, rs, slot, first, last):
+                arrive(6)
+                start(fetch(order(a0), 0))
+            step_a(a0, ab0, ab1, 0, True, False, [(g == 0, 1), (g == 1, 7)], order(a0 + 1))
+
+            def pair_a(i):
+                k = a0 + 2 * i + 1
+                more = 2 * i + 2 < na
+                step_a(k, ab1, ab0, 1, False, False, [(k == 3, 4)], jnp.where(more, order(k + 1), order_s(s0)))
+
+                @pl.when(i > 0)
+                def _():
+                    relay(k - 3)
+                    relay(k - 2)
+
+                @pl.when(more)
+                def _():
+                    step_a(k + 1, ab0, ab1, 0, False, False, [(k == 3, 5)], order(k + 2))
+
+                @pl.when(jnp.logical_not(more))
+                def _():
+                    step_a(k + 1, ab0, ab1, 0, False, True)
+
+            def body_a(i, _):
+                @pl.when(2 * i + 1 < na)
+                def _():
+                    pair_a(i)
+                return 0
+
+            lax.fori_loop(0, nblk // 2, body_a, 0)
+            relay(a0 + na - 2)
+
+            @pl.when(first_sweep)
+            def _():
+                relay(a0 + na - 1)
+
+        def step_s(place, rd, rs, slot, first, last):
+            j = order_s(place)
             if not last:
                 settle(j)
             if not first:
-                wait(fetch(j - 1, slot))
+                wait(fetch(j, slot))
                 if not last:
                     start(fetch(j, 1 - slot))
             for u in range(4):
@@ -273,24 +287,60 @@
                     sl = slice(u * (d // 4), (u + 1) * (d // 4))
                     S[:, sl] += jnp.dot(rs[...], xbuf[slot, :, sl], preferred_element_type=F32)
 
-        step_s(0, rb0, rb1, 1, True, False)
-
-        def body_s(i, _):
-            step_s(2 * i + 1, rb1, rb0, 0, False, False)
-
-            @pl.when(jnp.logical_and(i == 0, t > 0))
+        def rounds(g):
+            a0, s0 = 6 * g, 4 * g
+            na = jnp.where(first_sweep, 6 - 4 * g, nblk)
+            ns = jnp.where(first_sweep, nblk // 2, nblk)
+            rounds_a(g, a0, na, s0)
+
+            @pl.when(g == 0)
             def _():
-                relay(nblk - 1)
-
-            @pl.when(jnp.logical_and(i == 0, t == sweeps - 1))
+                S[...] = jnp.zeros_like(S)
+            step_s(s0, rb0, rb1, 1, True, False)
+
+            def pair_s(i):
+                j = s0 + 2 * i + 1
+                more = 2 * i + 2 < ns
+                step_s(j, rb1, rb0, 0, False, False)
+
+                @pl.when(jnp.logical_and(i == 0, t > 0))
+                def _():
+                    relay(nblk - 1)
+
+                @pl.when(jnp.logical_and(i == 0, t == sweeps - 1))
+                def _():
+                    bulk(1).start()
+
+                for v in (0, 1):
+                    @pl.when(jnp.logical_and(jnp.logical_and(first_sweep, g == 0), i == v))
+                    def _():
+                        take_py(5 + v)
+                        take_pz(4 + v)
+
+                @pl.when(more)
+                def _():
+                    step_s(j + 1, rb0, rb1, 1, False, False)
+
+                @pl.when(jnp.logical_not(more))
+                def _():
+                    step_s(j + 1, rb0, rb1, 1, False, True)
+
+            def body_s(i, _):
+                @pl.when(2 * i + 1 < ns)
+                def _():
+                    pair_s(i)
+                return 0
+
+            lax.fori_loop(0, nblk // 2, body_s, 0)
+
+        def body_r(g, _):
+            @pl.when(jnp.logical_or(first_sweep, g == 0))
             def _():
-                bulk(1).start()
-            step_s(2 * i + 2, rb0, rb1, 1, False, False)
+                rounds(g)
             return 0
 
-        lax.fori_loop(0, nblk // 2 - 1, body_s, 0)
-        step_s(nblk - 1, rb1, rb0, 0, False, False)
-        step_s(nblk, rb0, rb1, 1, False, True)
+        lax.fori_loop(0, 2, body_r, 0)
+
         def finish(g, _):
             r = pl.ds(pl.multiple_of(g * 64, 64), 64)
             n = jnp.sum(nacc[r, :], axis=1, keepdims=True)

time: 286 us -> 298 us (1.042)
  Pallas kernels: 266 us -> 278 us
    pallas_call x1, Pallas kernels: 266 us -> 278 us  [per_device(): pl.pallas_call(em_kernel, out_shape=(jax.ShapeDtypeStruct((k_loc, d), F32...]
where the time goes in v3:
time: 298 us
  Pallas kernels  278 us (93%)
  local copies, waits for them, and re-layouts  15.5 us (5%)
  other arithmetic  3.81 us (1%)
    pallas_call x1, Pallas kernels, per_device(): pl.pallas_call(em_kernel, out_shape=(jax.ShapeDtypeStruct((k_loc, d), F32...  278 us
    unnamed x5, local copies, waits for them, and re-layouts  13.2 us

profile of v3, /device:TPU:0, one launch (start us, length us, event | category | flops | bytes accessed | tf_op | source)
XLA Modules:
  0.0 297.9 jit_solution(17346150285754072479)
XLA Ops:
  0.6 0.7 dynamic_slice.3
  1.3 3.1 %multiply_reduce_fusion = f32[2048]{0:T(1024)S(1)} fusion(bf16[2048,1024]{1,0:T(8,128)(2,1)} %x_in.1), kind=kLoop, calls=%fused_computation | loop fusion | flops 6289408 | bytes 4202496 | tf_op jit(solution)/shard_map/reduce_sum | solution.py:461
  4.4 0.6 reshape.23.q_in
  5.1 1.0 broadcast_in_dim.2.lw_in
  6.1 278.0 %em_sweeps.1 = (f32[4096,1024]{1,0:T(8,128)}, f32[4,8,128]{2,1,0:T(8,128)}, f32[2,1,1024]{2,1,0:T(1,128)}, bf16[8192,1024]{1,0:T(8,128)(2,1)}) custom-call(f32[3]{0:T(128)} %beta.1, bf16[2048,1024]{1,0:T(8,128)(2,1)} %x_in.1, f32[4096,1024]{1,0:T(8,128)} %mu_in.1, f32[1024,128]{1,0:T(8,128)} %broadcast_in_dim.2.lw_in, f32[2,1,1024]{2,1,0:T(1,128)} %reshape.23.q_in), custom_call_target="tpu_custom_call" | custom-call | tf_op jit(solution)/shard_map/em_sweeps/pallas_call | solution.py:466
  284.0 0.7 reduce
  284.8 0.6 copy.9
  285.4 0.0 copy-start
  285.4 12.0 %copy.12 = f32[4096,1024]{1,0:T(8,128)} copy(f32[4096,1024]{1,0:T(8,128)} %get-tuple-element.12) | data formatting | bytes 33554432
  297.3 0.0 copy-done
  297.3 0.6 copy.13
  (3 shorter events, 0.0 us)
Async XLA Ops:
  285.4 12.0 %copy-start = (f32[4,8,128]{2,1,0:T(8,128)S(1)}, f32[4,8,128]{2,1,0:T(8,128)}, u32[]{:S(2)}) copy-start(f32[4,8,128]{2,1,0:T(8,128)} %get-tuple-element.7) | copy-start | bytes 49156

commit v4 on v2

--- a/solution.py
+++ b/solution.py
@@ -103,9 +103,12 @@
     def arrive(n):
         if n == 2:
             sib.wait_recv()
+            take_py(0)
+        elif n == 3:
+            take_py(1)
         elif n == 4:
-            take_py(0)
-            for i in range(1, 5):
+            take_pz(0)
+            for i in range(2, 5):
                 take_py(i)
                 take_pz(i - 1)
         elif n == 6:
@@ -234,7 +237,7 @@
             def _():
                 relay(2 * i - 2)
                 relay(2 * i - 1)
-            step_a(2 * i + 2, ab0, ab1, 0, False, False, [(i == 1, 5), (i == 2, 7)])
+            step_a(2 * i + 2, ab0, ab1, 0, False, False, [(i == 0, 3), (i == 1, 5), (i == 2, 7)])
             return 0
 
         lax.fori_loop(0, nblk // 2 - 1, body_a, 0)

time: 286 us -> 279 us (0.976)
  Pallas kernels: 266 us -> 259 us
    pallas_call x1, Pallas kernels: 266 us -> 259 us  [per_device(): pl.pallas_call(em_kernel, out_shape=(jax.ShapeDtypeStruct((k_loc, d), F32...]
where the time goes in v4:
time: 279 us
  Pallas kernels  259 us (93%)
  local copies, waits for them, and re-layouts  15.5 us (6%)
  other arithmetic  3.81 us (1%)
    pallas_call x1, Pallas kernels, per_device(): pl.pallas_call(em_kernel, out_shape=(jax.ShapeDtypeStruct((k_loc, d), F32...  259 us
    unnamed x5, local copies, waits for them, and re-layouts  13.2 us

profile of v4, /device:TPU:0, one launch (start us, length us, event | category | flops | bytes accessed | tf_op | source)
XLA Modules:
  0.0 278.9 jit_solution(15907678348328202279)
XLA Ops:
  0.6 0.7 dynamic_slice.3
  1.3 3.1 %multiply_reduce_fusion = f32[2048]{0:T(1024)S(1)} fusion(bf16[2048,1024]{1,0:T(8,128)(2,1)} %x_in.1), kind=kLoop, calls=%fused_computation | loop fusion | flops 6289408 | bytes 4202496 | tf_op jit(solution)/shard_map/reduce_sum | solution.py:414
  4.4 0.6 reshape.23.q_in
  5.1 1.0 broadcast_in_dim.2.lw_in
  6.1 259.0 %em_sweeps.1 = (f32[4096,1024]{1,0:T(8,128)}, f32[4,8,128]{2,1,0:T(8,128)}, f32[2,1,1024]{2,1,0:T(1,128)}, bf16[8192,1024]{1,0:T(8,128)(2,1)}) custom-call(f32[3]{0:T(128)} %beta.1, bf16[2048,1024]{1,0:T(8,128)(2,1)} %x_in.1, f32[4096,1024]{1,0:T(8,128)} %mu_in.1, f32[1024,128]{1,0:T(8,128)} %broadcast_in_dim.2.lw_in, f32[2,1,1024]{2,1,0:T(1,128)} %reshape.23.q_in), custom_call_target="tpu_custom_call" | custom-call | tf_op jit(solution)/shard_map/em_sweeps/pallas_call | solution.py:419
  265.0 0.7 reduce
  265.8 0.6 copy.9
  266.4 0.0 copy-start
  266.4 12.0 %copy.12 = f32[4096,1024]{1,0:T(8,128)} copy(f32[4096,1024]{1,0:T(8,128)} %get-tuple-element.12) | data formatting | bytes 33554432
  278.3 0.0 copy-done
  278.3 0.6 copy.13
  (3 shorter events, 0.0 us)
Async XLA Ops:
  266.4 12.0 %copy-start = (f32[4,8,128]{2,1,0:T(8,128)S(1)}, f32[4,8,128]{2,1,0:T(8,128)}, u32[]{:S(2)}) copy-start(f32[4,8,128]{2,1,0:T(8,128)} %get-tuple-element.7) | copy-start | bytes 49156
